TPU v7x, 32 devices: a whole 2x2x4 slice. The times are simulated.
32 devices in a mesh: gx: 8 (over z, y), gy: 4 (over x, core).
Axes of the slice: x: 2, y: 2, z: 4, core: 2. Of those that a mesh axis runs over, the one named last changes fastest.
Arguments:
- liquid_starting_warmth: float32 [32, 64, 1024], P('gx', 'gy'), may hold values from -6 to 6
- liquid_spreading_ratios: float32 [32, 64, 1024], P('gx', 'gy'), may hold values from 0.02 to 0.12
- liquid_advective_ratios: float32 [3, 32, 64, 1024], P(None, 'gx', 'gy'), may hold values from -0.08 to 0.08
- liquid_refresh_flags: int32 [32, 64, 8], P('gx', 'gy'), may hold values 0 or 1
- wall_starting_warmth: float32 [32, 64, 1024], P('gx', 'gy'), may hold values from -6 to 6
- wall_thermal_capacity: float32 [32, 64, 1024], P('gx', 'gy'), may hold values from 0.5 to 2
- thermal_conductance: float32 [32, 64, 1024], P('gx', 'gy'), may hold values from 0.5 to 15
- wall_energy_output: float32 [32, 64, 1024], P('gx', 'gy'), may hold values from -36 to 36
- coupling_partner_lookup: int32 [32, 64], P('gx', 'gy'), may hold values from 0 to 63, each once within a row
Outputs:
- fluid_after: float32 [32, 64, 1024], P('gx', 'gy')
- solid_after: float32 [32, 64, 1024], P('gx', 'gy')
Inputs may be any that keep to these rules, and one draw needn't show every extreme that they name: For each first index, the row of coupling_partner_lookup holds every number of 0 to 63 once.
All inputs are finite; a program needn't handle non-finite values. No bound on the sum of `liquid_refresh_flags` on one device may be relied on, other than what follows from the above.
Results may differ from a plain program's by a relative error of at most 0.00023.
Values sent between devices are 32-bit elements; how exact they have to be, the bound alone decides.
A program may use at most 64 MiB of HBM per device.

v0:
```python
import jax
import jax.numpy as jnp
from jax import lax
from jax.sharding import PartitionSpec as P

SUBSTEPS = 4
ITERS = 4
ZB = 128


def padded_2(cells, sides, width):
    for axis, dim in sides:
        count = lax.axis_size(axis)
        ends = count - 1
        head = lax.slice_in_dim(cells, 0, width, axis=dim)
        tail = lax.slice_in_dim(cells, cells.shape[dim] - width, cells.shape[dim], axis=dim)
        cells = jnp.concatenate(
            [
                lax.ppermute(tail, axis, [(i, (i + 1) % count) for i in range(ends)]),
                cells,
                lax.ppermute(head, axis, [((i + 1) % count, i) for i in range(ends)]),
            ],
            axis=dim,
        )
    return cells


def advance(current_estimate, padded, ghost_row, diffusion, velocity, active_cells):
    below = jnp.concatenate([ghost_row[:, :, None], current_estimate[:, :, :-1]], axis=2)
    above = jnp.concatenate(
        [current_estimate[:, :, 1:], jnp.zeros_like(current_estimate[:, :, :1])], axis=2
    )
    couples = (
        (padded[:-2, 1:-1], padded[2:, 1:-1]),
        (padded[1:-1, :-2], padded[1:-1, 2:]),
        (below, above),
    )
    spread = -6.0 * current_estimate
    carried = jnp.zeros_like(current_estimate)
    for component in range(3):
        behind, ahead = couples[component]
        spread = spread + behind + ahead
        flow_speed = velocity[component]
        carried = (
            carried
            + jnp.maximum(flow_speed, 0.0) * (current_estimate - behind)
            + jnp.minimum(flow_speed, 0.0) * (ahead - current_estimate)
        )
    return current_estimate + active_cells * (diffusion * spread - carried)


def neighbours(field, padded):
    below = jnp.concatenate([jnp.zeros_like(field[:, :, :1]), field[:, :, :-1]], axis=2)
    above = jnp.concatenate([field[:, :, 1:], jnp.zeros_like(field[:, :, :1])], axis=2)
    return (padded[:-2, 1:-1], padded[2:, 1:-1], padded[1:-1, :-2], padded[1:-1, 2:], below, above)


def thermal_flow_operator(field, padded_field, thermal_conductance, bordered_conductance, capacity):
    accumulated = capacity * field
    for near_value, near_cond in zip(
        neighbours(field, padded_field), neighbours(thermal_conductance, bordered_conductance)
    ):
        accumulated = accumulated + 0.5 * (thermal_conductance + near_cond) * (field - near_value)
    return accumulated


def diagonal_of(thermal_conductance, bordered_conductance, capacity):
    accumulated = capacity
    for near_cond in neighbours(thermal_conductance, bordered_conductance):
        accumulated = accumulated + 0.5 * (thermal_conductance + near_cond)
    return accumulated


def local(
    liquid_starting_warmth,
    liquid_spreading_ratios,
    liquid_advective_ratios,
    liquid_refresh_flags,
    wall_starting_warmth,
    wall_thermal_capacity,
    thermal_conductance,
    wall_energy_output,
    coupling_partner_lookup,
):
    local_cols = coupling_partner_lookup.shape[1]
    topmost_layers = lax.all_gather(wall_starting_warmth[:, :, -1], "gy", axis=1, tiled=True)
    positions = jnp.arange(topmost_layers.shape[1], dtype=jnp.int32)
    picks = coupling_partner_lookup[:, :, None] == positions[None, None, :]
    ghost_row = jnp.sum(jnp.where(picks, topmost_layers[:, None, :], 0.0), axis=2)
    active_cells = jnp.repeat(liquid_refresh_flags.astype(jnp.float32), ZB, axis=2)
    padded_fluid, bordered_wall_warmth, bordered_conductance = (
        padded_2(liquid_starting_warmth, (("gx", 0), ("gy", 1)), 1),
        padded_2(wall_starting_warmth, (("gx", 0), ("gy", 1)), 1),
        padded_2(thermal_conductance, (("gx", 0), ("gy", 1)), 1),
    )
    current_estimate = liquid_starting_warmth
    padded = padded_fluid
    flux_sum = jnp.zeros_like(ghost_row)
    for substep in range(SUBSTEPS):
        flux_sum = flux_sum + (current_estimate[:, :, 0] - ghost_row)
        if substep > 0:
            padded = padded_2(current_estimate, (("gx", 0), ("gy", 1)), 1)
        current_estimate = advance(
            current_estimate,
            padded,
            ghost_row,
            liquid_spreading_ratios,
            liquid_advective_ratios,
            active_cells,
        )
    flux_mean = flux_sum / SUBSTEPS
    map_wide = lax.all_gather(coupling_partner_lookup, "gy", axis=1, tiled=True)
    flux_wide = lax.all_gather(flux_mean, "gy", axis=1, tiled=True)
    own_cols = lax.axis_index("gy") * local_cols + jnp.arange(local_cols, dtype=jnp.int32)
    owners = map_wide[:, None, :] == own_cols[None, :, None]
    arrived = jnp.sum(jnp.where(owners, flux_wide[:, None, :], 0.0), axis=2)
    equation_source_term = wall_thermal_capacity * wall_starting_warmth + wall_energy_output
    equation_source_term = equation_source_term.at[:, :, -1].add(arrived)
    diagonal = diagonal_of(thermal_conductance, bordered_conductance, wall_thermal_capacity)

    def apply_stiffness_matrix(field, padded_field):
        return thermal_flow_operator(
            field, padded_field, thermal_conductance, bordered_conductance, wall_thermal_capacity
        )

    def rimmed(field):
        return padded_2(field, (("gx", 0), ("gy", 1)), 1)

    converged_warmth = wall_starting_warmth
    leftover_error = equation_source_term - apply_stiffness_matrix(
        converged_warmth, bordered_wall_warmth
    )
    scaled = leftover_error / diagonal

    def paired(residual_now, scaled_now, image_now):
        return lax.psum(
            (jnp.sum(residual_now * scaled_now), jnp.sum(scaled_now * image_now)), ("gx", "gy")
        )

    image = apply_stiffness_matrix(scaled, rimmed(scaled))
    inner_rz, curvature = paired(leftover_error, scaled, image)
    descent_length = inner_rz / curvature
    search_heading = scaled
    image_dir = image
    for iteration in range(ITERS):
        converged_warmth = converged_warmth + descent_length * search_heading
        leftover_error = leftover_error - descent_length * image_dir
        if iteration + 1 < ITERS:
            scaled = leftover_error / diagonal
            image = apply_stiffness_matrix(scaled, rimmed(scaled))
            inner_next, curvature = paired(leftover_error, scaled, image)
            ratio = inner_next / inner_rz
            descent_length = inner_next / (curvature - ratio * inner_next / descent_length)
            search_heading = scaled + ratio * search_heading
            image_dir = image + ratio * image_dir
            inner_rz = inner_next
    return (current_estimate, converged_warmth)


def solution(mesh):
    return jax.shard_map(
        local,
        mesh=mesh,
        in_specs=(
            P("gx", "gy", None),
            P("gx", "gy", None),
            P(None, "gx", "gy", None),
            P("gx", "gy", None),
            P("gx", "gy", None),
            P("gx", "gy", None),
            P("gx", "gy", None),
            P("gx", "gy", None),
            P("gx", "gy"),
        ),
        out_specs=(P("gx", "gy", None), P("gx", "gy", None)),
        check_vma=False,
    )
```

profile of v0, /device:TPU:0, one launch (start us, length us, event | category | flops | bytes accessed | tf_op | source)
XLA Modules:
  0.0 360.6 jit_solution(3652510717344675397)
XLA Ops:
  1.6 4.9 %collective-permute-start = (f32[1,16,1024]{2,1,0:T(8,128)S(1)}, f32[1,16,1024]{2,1,0:T(8,128)S(1)}, u32[]{:S(2)}, u32[]{:S(2)}) collective-permute-start(f32[1,16,1024]{2,1,0:T(8,128)S(1)} %get-tuple-element.112), channel_id=1, source_target_pairs={{0,4},{4,8},{8,12},{12,16},{16,20},{20,24},{24,28},{1,5},{5,9},{9,... | collective-permute-start | bytes 196616 | tf_op jit(solution)/shard_map/ppermute | solution.py:19
  9.3 5.2 %collective-permute-start.17 = (f32[1,16,1024]{2,1,0:T(8,128)S(1)}, f32[1,16,1024]{2,1,0:T(8,128)S(1)}, u32[]{:S(2)}, u32[]{:S(2)}) collective-permute-start(f32[1,16,1024]{2,1,0:T(8,128)S(1)} %get-tuple-element.91), channel_id=1, source_target_pairs={{0,4},{4,8},{8,12},{12,16},{16,20},{20,24},{24,28},{1,5},{5,9},{9,... | collective-permute-start | bytes 196616 | tf_op jit(solution)/shard_map/ppermute | solution.py:19
  14.5 4.8 %collective-permute-start.16 = (f32[1,16,1024]{2,1,0:T(8,128)S(1)}, f32[1,16,1024]{2,1,0:T(8,128)S(1)}, u32[]{:S(2)}, u32[]{:S(2)}) collective-permute-start(f32[1,16,1024]{2,1,0:T(8,128)S(1)} %get-tuple-element.96), channel_id=1, source_target_pairs={{0,4},{4,8},{8,12},{12,16},{16,20},{20,24},{24,28},{1,5},{5,9},{9,... | collective-permute-start | bytes 196616 | tf_op jit(solution)/shard_map/ppermute | solution.py:19
  22.1 5.3 %all-gather.1 = s32[4,16,4]{1,2,0:T(4,128)S(1)} all-gather(s32[1,16,4]{1,2,0:T(4,128)S(1)} %bitcast.80), channel_id=1, replica_groups=mesh['gx'=8,'gy'=4] {'gy'}, dimensions={0}, use_global_device_ids=true | all-gather | bytes 1280 | tf_op jit(solution)/shard_map/all_gather | solution.py:112
  27.6 5.4 %all-gather = f32[4,64,1]{2,1,0:T(8,128)S(1)} all-gather(f32[4,16,1]{2,1,0:T(8,128)S(1)} %slice.433), channel_id=2, replica_groups=mesh['gx'=8,'gy'=4] {'gy'}, dimensions={1}, use_global_device_ids=true | all-gather | bytes 1280 | tf_op jit(solution)/shard_map/all_gather | solution.py:86
  34.9 4.9 %collective-permute-done.18 = f32[1,16,1024]{2,1,0:T(8,128)S(1)} collective-permute-done((f32[1,16,1024]{2,1,0:T(8,128)S(1)}, f32[1,16,1024]{2,1,0:T(8,128)S(1)}, u32[]{:S(2)}, u32[]{:S(2)}) %collective-permute-start.18) | collective-permute-done | bytes 65568 | tf_op jit(solution)/shard_map/ppermute | solution.py:21
  41.2 3.0 collective-permute-start.20
  44.4 3.1 collective-permute-start.2
  49.7 3.0 collective-permute-start.21
  53.2 4.3 %collective-permute-start.4 = (f32[1,16,1024]{2,1,0:T(8,128)S(1)}, f32[1,16,1024]{2,1,0:T(8,128)S(1)}, u32[]{:S(2)}, u32[]{:S(2)}) collective-permute-start(f32[1,16,1024]{2,1,0:T(8,128)S(1)} %get-tuple-element.108), channel_id=1, source_target_pairs={{0,4},{4,8},{8,12},{12,16},{16,20},{20,24},{24,28},{1,5},{5,9},{9,... | collective-permute-start | bytes 196616 | tf_op jit(solution)/shard_map/ppermute | solution.py:19
  59.4 4.5 %collective-permute-done.5 = f32[1,16,1024]{2,1,0:T(8,128)S(1)} collective-permute-done((f32[1,16,1024]{2,1,0:T(8,128)S(1)}, f32[1,16,1024]{2,1,0:T(8,128)S(1)}, u32[]{:S(2)}, u32[]{:S(2)}) %collective-permute-start.5) | collective-permute-done | bytes 65568 | tf_op jit(solution)/shard_map/ppermute | solution.py:21
  70.4 3.4 collective-permute-start.8
  75.7 4.3 %collective-permute-done.9 = f32[1,16,1024]{2,1,0:T(8,128)S(1)} collective-permute-done((f32[1,16,1024]{2,1,0:T(8,128)S(1)}, f32[1,16,1024]{2,1,0:T(8,128)S(1)}, u32[]{:S(2)}, u32[]{:S(2)}) %collective-permute-start.9) | collective-permute-done | bytes 65568 | tf_op jit(solution)/shard_map/ppermute | solution.py:21
  80.0 3.0 collective-permute-start.10
  87.6 6.6 %all-gather.2 = f32[4,16,4]{1,2,0:T(4,128)S(1)} all-gather(f32[1,16,4]{1,2,0:T(4,128)S(1)} %multiply_bitcast_fusion), channel_id=1, replica_groups=mesh['gx'=8,'gy'=4] {'gy'}, dimensions={0}, use_global_device_ids=true | all-gather | bytes 1280 | tf_op jit(solution)/shard_map/all_gather | solution.py:113
  95.7 2.8 fusion.162
  98.5 4.3 %collective-permute-start.24 = (f32[1,16,1024]{2,1,0:T(8,128)S(1)}, f32[1,16,1024]{2,1,0:T(8,128)S(1)}, u32[]{:S(2)}, u32[]{:S(2)}) collective-permute-start(f32[1,16,1024]{2,1,0:T(8,128)S(1)} %get-tuple-element.84), channel_id=1, source_target_pairs={{0,4},{4,8},{8,12},{12,16},{16,20},{20,24},{24,28},{1,5},{5,9},{9,... | collective-permute-start | bytes 196616 | tf_op jit(solution)/shard_map/ppermute | solution.py:19
  105.0 4.0 %collective-permute-done.25 = f32[1,16,1024]{2,1,0:T(8,128)S(1)} collective-permute-done((f32[1,16,1024]{2,1,0:T(8,128)S(1)}, f32[1,16,1024]{2,1,0:T(8,128)S(1)}, u32[]{:S(2)}, u32[]{:S(2)}) %collective-permute-start.25) | collective-permute-done | bytes 65568 | tf_op jit(solution)/shard_map/ppermute | solution.py:21
  111.8 3.4 collective-permute-done.27
  117.0 41.0 %all-reduce.19 = (f32[]{:T(128)}, f32[]{:T(128)}) all-reduce(f32[]{:T(128)} %get-tuple-element.27, f32[]{:T(128)} %get-tuple-element.26), channel_id=1, replica_groups=mesh['gx'=8,'gy'=4] {'gx','gy'}, use_global_device_ids=true, to_apply=%region_3.4 | all-reduce | flops 2 | bytes 16 | tf_op jit(solution)/shard_map/psum | solution.py:136
  160.4 4.4 %collective-permute-start.28 = (f32[1,16,1024]{2,1,0:T(8,128)S(1)}, f32[1,16,1024]{2,1,0:T(8,128)S(1)}, u32[]{:S(2)}, u32[]{:S(2)}) collective-permute-start(f32[1,16,1024]{2,1,0:T(8,128)S(1)} %get-tuple-element.80), channel_id=1, source_target_pairs={{0,4},{4,8},{8,12},{12,16},{16,20},{20,24},{24,28},{1,5},{5,9},{9,... | collective-permute-start | bytes 196616 | tf_op jit(solution)/shard_map/ppermute | solution.py:19
  166.7 5.2 %collective-permute-start.12 = (f32[1,16,1024]{2,1,0:T(8,128)}, f32[1,16,1024]{2,1,0:T(8,128)}, u32[]{:S(2)}, u32[]{:S(2)}) collective-permute-start(f32[1,16,1024]{2,1,0:T(8,128)} %get-tuple-element.100), channel_id=1, source_target_pairs={{0,4},{4,8},{8,12},{12,16},{16,20},{20,24},{24,28},{1,5},{5,9},{9,... | collective-permute-start | bytes 196616 | tf_op jit(solution)/shard_map/ppermute | solution.py:19
  176.1 2.9 collective-permute-done.31
  180.8 42.0 %all-reduce.18 = (f32[]{:T(128)}, f32[]{:T(128)}) all-reduce(f32[]{:T(128)} %get-tuple-element.25, f32[]{:T(128)} %get-tuple-element.24), channel_id=1, replica_groups=mesh['gx'=8,'gy'=4] {'gx','gy'}, use_global_device_ids=true, to_apply=%region_7.8 | all-reduce | flops 2 | bytes 16 | tf_op jit(solution)/shard_map/psum | solution.py:136
  228.3 4.4 %collective-permute-start.32 = (f32[1,16,1024]{2,1,0:T(8,128)S(1)}, f32[1,16,1024]{2,1,0:T(8,128)S(1)}, u32[]{:S(2)}, u32[]{:S(2)}) collective-permute-start(f32[1,16,1024]{2,1,0:T(8,128)S(1)} %get-tuple-element.76), channel_id=1, source_target_pairs={{0,4},{4,8},{8,12},{12,16},{16,20},{20,24},{24,28},{1,5},{5,9},{9,... | collective-permute-start | bytes 196616 | tf_op jit(solution)/shard_map/ppermute | solution.py:19
  238.9 4.5 %collective-permute-start.34 = (f32[6,1,1024]{2,1,0:T(1,128)S(1)}, f32[6,1,1024]{2,1,0:T(1,128)S(1)}, u32[]{:S(2)}, u32[]{:S(2)}) collective-permute-start(f32[6,1,1024]{2,1,0:T(1,128)S(1)} %get-tuple-element.54), channel_id=1, source_target_pairs={{0,1},{1,2},{2,3},{4,5},{5,6},{6,7},{8,9},{9,10},{10,11},{12,13},{... | collective-permute-start | bytes 73736 | tf_op jit(solution)/shard_map/ppermute | solution.py:19
  245.0 2.9 collective-permute-done.35
  249.6 41.4 %all-reduce.17 = (f32[]{:T(128)}, f32[]{:T(128)}) all-reduce(f32[]{:T(128)} %get-tuple-element.23, f32[]{:T(128)} %get-tuple-element.22), channel_id=1, replica_groups=mesh['gx'=8,'gy'=4] {'gx','gy'}, use_global_device_ids=true, to_apply=%region_11.12 | all-reduce | flops 2 | bytes 16 | tf_op jit(solution)/shard_map/psum | solution.py:136
  296.8 4.6 %collective-permute-start.36 = (f32[1,16,1024]{2,1,0:T(8,128)S(1)}, f32[1,16,1024]{2,1,0:T(8,128)S(1)}, u32[]{:S(2)}, u32[]{:S(2)}) collective-permute-start(f32[1,16,1024]{2,1,0:T(8,128)S(1)} %get-tuple-element.74), channel_id=1, source_target_pairs={{0,4},{4,8},{8,12},{12,16},{16,20},{20,24},{24,28},{1,5},{5,9},{9,... | collective-permute-start | bytes 196616 | tf_op jit(solution)/shard_map/ppermute | solution.py:19
  304.7 2.8 collective-permute-done.37
  310.5 3.3 collective-permute-done.39
  314.8 41.4 %all-reduce.16 = (f32[]{:T(128)}, f32[]{:T(128)}) all-reduce(f32[]{:T(128)} %get-tuple-element.36, f32[]{:T(128)} %fusion.6), channel_id=1, replica_groups=mesh['gx'=8,'gy'=4] {'gx','gy'}, use_global_device_ids=true, to_apply=%region_15.16 | all-reduce | flops 2 | bytes 16 | tf_op jit(solution)/shard_map/psum | solution.py:136
  (199 shorter events, 64.8 us)
Async XLA Ops:
  1.6 39.6 %collective-permute-start = (f32[1,16,1024]{2,1,0:T(8,128)S(1)}, f32[1,16,1024]{2,1,0:T(8,128)S(1)}, u32[]{:S(2)}, u32[]{:S(2)}) collective-permute-start(f32[1,16,1024]{2,1,0:T(8,128)S(1)} %get-tuple-element.112), channel_id=1, source_target_pairs={{0,4},{4,8},{8,12},{12,16},{16,20},{20,24},{24,28},{1,5},{5,9},{9,... | collective-permute-start | bytes 196616 | tf_op jit(solution)/shard_map/ppermute | solution.py:19
  6.5 37.8 %collective-permute-start.1 = (f32[1,16,1024]{2,1,0:T(8,128)S(1)}, f32[1,16,1024]{2,1,0:T(8,128)S(1)}, u32[]{:S(2)}, u32[]{:S(2)}) collective-permute-start(f32[1,16,1024]{2,1,0:T(8,128)S(1)} %get-tuple-element.113), channel_id=1, source_target_pairs={{4,0},{8,4},{12,8},{16,12},{20,16},{24,20},{28,24},{5,1},{9,5},{13... | collective-permute-start | bytes 196616 | tf_op jit(solution)/shard_map/ppermute | solution.py:21
  8.0 41.0 %collective-permute-start.19 = (f32[1,16,1024]{2,1,0:T(8,128)S(1)}, f32[1,16,1024]{2,1,0:T(8,128)S(1)}, u32[]{:S(2)}, u32[]{:S(2)}) collective-permute-start(f32[1,16,1024]{2,1,0:T(8,128)S(1)} %get-tuple-element.90), channel_id=1, source_target_pairs={{4,0},{8,4},{12,8},{16,12},{20,16},{24,20},{28,24},{5,1},{9,5},{13... | collective-permute-start | bytes 196616 | tf_op jit(solution)/shard_map/ppermute | solution.py:21
  9.3 38.3 %collective-permute-start.17 = (f32[1,16,1024]{2,1,0:T(8,128)S(1)}, f32[1,16,1024]{2,1,0:T(8,128)S(1)}, u32[]{:S(2)}, u32[]{:S(2)}) collective-permute-start(f32[1,16,1024]{2,1,0:T(8,128)S(1)} %get-tuple-element.91), channel_id=1, source_target_pairs={{0,4},{4,8},{8,12},{12,16},{16,20},{20,24},{24,28},{1,5},{5,9},{9,... | collective-permute-start | bytes 196616 | tf_op jit(solution)/shard_map/ppermute | solution.py:19
  14.5 19.1 %collective-permute-start.16 = (f32[1,16,1024]{2,1,0:T(8,128)S(1)}, f32[1,16,1024]{2,1,0:T(8,128)S(1)}, u32[]{:S(2)}, u32[]{:S(2)}) collective-permute-start(f32[1,16,1024]{2,1,0:T(8,128)S(1)} %get-tuple-element.96), channel_id=1, source_target_pairs={{0,4},{4,8},{8,12},{12,16},{16,20},{20,24},{24,28},{1,5},{5,9},{9,... | collective-permute-start | bytes 196616 | tf_op jit(solution)/shard_map/ppermute | solution.py:19
  33.6 6.2 %collective-permute-start.18 = (f32[1,16,1024]{2,1,0:T(8,128)S(1)}, f32[1,16,1024]{2,1,0:T(8,128)S(1)}, u32[]{:S(2)}, u32[]{:S(2)}) collective-permute-start(f32[1,16,1024]{2,1,0:T(8,128)S(1)} %get-tuple-element.97), channel_id=1, source_target_pairs={{4,0},{8,4},{12,8},{16,12},{20,16},{24,20},{28,24},{5,1},{9,5},{13... | collective-permute-start | bytes 196616 | tf_op jit(solution)/shard_map/ppermute | solution.py:21
  39.9 55.1 %collective-permute-start.22 = (f32[6,1,1024]{2,1,0:T(1,128)S(1)}, f32[6,1,1024]{2,1,0:T(1,128)S(1)}, u32[]{:S(2)}, u32[]{:S(2)}) collective-permute-start(f32[6,1,1024]{2,1,0:T(1,128)S(1)} %get-tuple-element.60), channel_id=1, source_target_pairs={{1,0},{2,1},{3,2},{5,4},{6,5},{7,6},{9,8},{10,9},{11,10},{13,12},{... | collective-permute-start | bytes 73736 | tf_op jit(solution)/shard_map/ppermute | solution.py:21
  41.2 53.8 %collective-permute-start.20 = (f32[6,1,1024]{2,1,0:T(1,128)S(1)}, f32[6,1,1024]{2,1,0:T(1,128)S(1)}, u32[]{:S(2)}, u32[]{:S(2)}) collective-permute-start(f32[6,1,1024]{2,1,0:T(1,128)S(1)} %get-tuple-element.61), channel_id=1, source_target_pairs={{0,1},{1,2},{2,3},{4,5},{5,6},{6,7},{8,9},{9,10},{10,11},{12,13},{... | collective-permute-start | bytes 73736 | tf_op jit(solution)/shard_map/ppermute | solution.py:19
  44.4 8.3 %collective-permute-start.2 = (f32[6,1,1024]{2,1,0:T(1,128)S(1)}, f32[6,1,1024]{2,1,0:T(1,128)S(1)}, u32[]{:S(2)}, u32[]{:S(2)}) collective-permute-start(f32[6,1,1024]{2,1,0:T(1,128)S(1)} %get-tuple-element.70), channel_id=1, source_target_pairs={{0,1},{1,2},{2,3},{4,5},{5,6},{6,7},{8,9},{9,10},{10,11},{12,13},{... | collective-permute-start | bytes 73736 | tf_op jit(solution)/shard_map/ppermute | solution.py:19
  47.6 5.2 %collective-permute-start.3 = (f32[6,1,1024]{2,1,0:T(1,128)S(1)}, f32[6,1,1024]{2,1,0:T(1,128)S(1)}, u32[]{:S(2)}, u32[]{:S(2)}) collective-permute-start(f32[6,1,1024]{2,1,0:T(1,128)S(1)} %get-tuple-element.71), channel_id=1, source_target_pairs={{1,0},{2,1},{3,2},{5,4},{6,5},{7,6},{9,8},{10,9},{11,10},{13,12},{... | collective-permute-start | bytes 73736 | tf_op jit(solution)/shard_map/ppermute | solution.py:21
  49.7 45.4 %collective-permute-start.21 = (f32[6,1,1024]{2,1,0:T(1,128)S(1)}, f32[6,1,1024]{2,1,0:T(1,128)S(1)}, u32[]{:S(2)}, u32[]{:S(2)}) collective-permute-start(f32[6,1,1024]{2,1,0:T(1,128)S(1)} %get-tuple-element.62), channel_id=1, source_target_pairs={{0,1},{1,2},{2,3},{4,5},{5,6},{6,7},{8,9},{9,10},{10,11},{12,13},{... | collective-permute-start | bytes 73736 | tf_op jit(solution)/shard_map/ppermute | solution.py:19
  53.2 6.2 %collective-permute-start.4 = (f32[1,16,1024]{2,1,0:T(8,128)S(1)}, f32[1,16,1024]{2,1,0:T(8,128)S(1)}, u32[]{:S(2)}, u32[]{:S(2)}) collective-permute-start(f32[1,16,1024]{2,1,0:T(8,128)S(1)} %get-tuple-element.108), channel_id=1, source_target_pairs={{0,4},{4,8},{8,12},{12,16},{16,20},{20,24},{24,28},{1,5},{5,9},{9,... | collective-permute-start | bytes 196616 | tf_op jit(solution)/shard_map/ppermute | solution.py:19
  57.5 6.4 %collective-permute-start.5 = (f32[1,16,1024]{2,1,0:T(8,128)S(1)}, f32[1,16,1024]{2,1,0:T(8,128)S(1)}, u32[]{:S(2)}, u32[]{:S(2)}) collective-permute-start(f32[1,16,1024]{2,1,0:T(8,128)S(1)} %get-tuple-element.109), channel_id=1, source_target_pairs={{4,0},{8,4},{12,8},{16,12},{20,16},{24,20},{28,24},{5,1},{9,5},{13... | collective-permute-start | bytes 196616 | tf_op jit(solution)/shard_map/ppermute | solution.py:21
  70.4 5.3 %collective-permute-start.8 = (f32[1,16,1024]{2,1,0:T(8,128)S(1)}, f32[1,16,1024]{2,1,0:T(8,128)S(1)}, u32[]{:S(2)}, u32[]{:S(2)}) collective-permute-start(f32[1,16,1024]{2,1,0:T(8,128)S(1)} %get-tuple-element.104), channel_id=1, source_target_pairs={{0,4},{4,8},{8,12},{12,16},{16,20},{20,24},{24,28},{1,5},{5,9},{9,... | collective-permute-start | bytes 196616 | tf_op jit(solution)/shard_map/ppermute | solution.py:19
  73.8 6.2 %collective-permute-start.9 = (f32[1,16,1024]{2,1,0:T(8,128)S(1)}, f32[1,16,1024]{2,1,0:T(8,128)S(1)}, u32[]{:S(2)}, u32[]{:S(2)}) collective-permute-start(f32[1,16,1024]{2,1,0:T(8,128)S(1)} %get-tuple-element.105), channel_id=1, source_target_pairs={{4,0},{8,4},{12,8},{16,12},{20,16},{24,20},{28,24},{5,1},{9,5},{13... | collective-permute-start | bytes 196616 | tf_op jit(solution)/shard_map/ppermute | solution.py:21
  84.4 10.6 %collective-permute-start.23 = (f32[6,1,1024]{2,1,0:T(1,128)S(1)}, f32[6,1,1024]{2,1,0:T(1,128)S(1)}, u32[]{:S(2)}, u32[]{:S(2)}) collective-permute-start(f32[6,1,1024]{2,1,0:T(1,128)S(1)} %get-tuple-element.63), channel_id=1, source_target_pairs={{1,0},{2,1},{3,2},{5,4},{6,5},{7,6},{9,8},{10,9},{11,10},{13,12},{... | collective-permute-start | bytes 73736 | tf_op jit(solution)/shard_map/ppermute | solution.py:21
  98.5 6.5 %collective-permute-start.24 = (f32[1,16,1024]{2,1,0:T(8,128)S(1)}, f32[1,16,1024]{2,1,0:T(8,128)S(1)}, u32[]{:S(2)}, u32[]{:S(2)}) collective-permute-start(f32[1,16,1024]{2,1,0:T(8,128)S(1)} %get-tuple-element.84), channel_id=1, source_target_pairs={{0,4},{4,8},{8,12},{12,16},{16,20},{20,24},{24,28},{1,5},{5,9},{9,... | collective-permute-start | bytes 196616 | tf_op jit(solution)/shard_map/ppermute | solution.py:19
  102.9 6.2 %collective-permute-start.25 = (f32[1,16,1024]{2,1,0:T(8,128)S(1)}, f32[1,16,1024]{2,1,0:T(8,128)S(1)}, u32[]{:S(2)}, u32[]{:S(2)}) collective-permute-start(f32[1,16,1024]{2,1,0:T(8,128)S(1)} %get-tuple-element.85), channel_id=1, source_target_pairs={{4,0},{8,4},{12,8},{16,12},{20,16},{24,20},{28,24},{5,1},{9,5},{13... | collective-permute-start | bytes 196616 | tf_op jit(solution)/shard_map/ppermute | solution.py:21
  110.4 4.9 %collective-permute-start.27 = (f32[6,1,1024]{2,1,0:T(1,128)S(1)}, f32[6,1,1024]{2,1,0:T(1,128)S(1)}, u32[]{:S(2)}, u32[]{:S(2)}) collective-permute-start(f32[6,1,1024]{2,1,0:T(1,128)S(1)} %get-tuple-element.59), channel_id=1, source_target_pairs={{1,0},{2,1},{3,2},{5,4},{6,5},{7,6},{9,8},{10,9},{11,10},{13,12},{... | collective-permute-start | bytes 73736 | tf_op jit(solution)/shard_map/ppermute | solution.py:21
  160.4 12.8 %collective-permute-start.28 = (f32[1,16,1024]{2,1,0:T(8,128)S(1)}, f32[1,16,1024]{2,1,0:T(8,128)S(1)}, u32[]{:S(2)}, u32[]{:S(2)}) collective-permute-start(f32[1,16,1024]{2,1,0:T(8,128)S(1)} %get-tuple-element.80), channel_id=1, source_target_pairs={{0,4},{4,8},{8,12},{12,16},{16,20},{20,24},{24,28},{1,5},{5,9},{9,... | collective-permute-start | bytes 196616 | tf_op jit(solution)/shard_map/ppermute | solution.py:19
  164.8 8.4 %collective-permute-start.29 = (f32[1,16,1024]{2,1,0:T(8,128)S(1)}, f32[1,16,1024]{2,1,0:T(8,128)S(1)}, u32[]{:S(2)}, u32[]{:S(2)}) collective-permute-start(f32[1,16,1024]{2,1,0:T(8,128)S(1)} %get-tuple-element.81), channel_id=1, source_target_pairs={{4,0},{8,4},{12,8},{16,12},{20,16},{24,20},{28,24},{5,1},{9,5},{13... | collective-permute-start | bytes 196616 | tf_op jit(solution)/shard_map/ppermute | solution.py:21
  166.7 67.2 %collective-permute-start.12 = (f32[1,16,1024]{2,1,0:T(8,128)}, f32[1,16,1024]{2,1,0:T(8,128)}, u32[]{:S(2)}, u32[]{:S(2)}) collective-permute-start(f32[1,16,1024]{2,1,0:T(8,128)} %get-tuple-element.100), channel_id=1, source_target_pairs={{0,4},{4,8},{8,12},{12,16},{16,20},{20,24},{24,28},{1,5},{5,9},{9,... | collective-permute-start | bytes 196616 | tf_op jit(solution)/shard_map/ppermute | solution.py:19
  171.9 62.1 %collective-permute-start.13 = (f32[1,16,1024]{2,1,0:T(8,128)}, f32[1,16,1024]{2,1,0:T(8,128)}, u32[]{:S(2)}, u32[]{:S(2)}) collective-permute-start(f32[1,16,1024]{2,1,0:T(8,128)} %get-tuple-element.101), channel_id=1, source_target_pairs={{4,0},{8,4},{12,8},{16,12},{20,16},{24,20},{28,24},{5,1},{9,5},{13... | collective-permute-start | bytes 196616 | tf_op jit(solution)/shard_map/ppermute | solution.py:21
  174.6 4.5 %collective-permute-start.31 = (f32[6,1,1024]{2,1,0:T(1,128)S(1)}, f32[6,1,1024]{2,1,0:T(1,128)S(1)}, u32[]{:S(2)}, u32[]{:S(2)}) collective-permute-start(f32[6,1,1024]{2,1,0:T(1,128)S(1)} %get-tuple-element.57), channel_id=1, source_target_pairs={{1,0},{2,1},{3,2},{5,4},{6,5},{7,6},{9,8},{10,9},{11,10},{13,12},{... | collective-permute-start | bytes 73736 | tf_op jit(solution)/shard_map/ppermute | solution.py:21
  228.3 10.4 %collective-permute-start.32 = (f32[1,16,1024]{2,1,0:T(8,128)S(1)}, f32[1,16,1024]{2,1,0:T(8,128)S(1)}, u32[]{:S(2)}, u32[]{:S(2)}) collective-permute-start(f32[1,16,1024]{2,1,0:T(8,128)S(1)} %get-tuple-element.76), channel_id=1, source_target_pairs={{0,4},{4,8},{8,12},{12,16},{16,20},{20,24},{24,28},{1,5},{5,9},{9,... | collective-permute-start | bytes 196616 | tf_op jit(solution)/shard_map/ppermute | solution.py:19
  232.7 6.2 %collective-permute-start.33 = (f32[1,16,1024]{2,1,0:T(8,128)S(1)}, f32[1,16,1024]{2,1,0:T(8,128)S(1)}, u32[]{:S(2)}, u32[]{:S(2)}) collective-permute-start(f32[1,16,1024]{2,1,0:T(8,128)S(1)} %get-tuple-element.77), channel_id=1, source_target_pairs={{4,0},{8,4},{12,8},{16,12},{20,16},{24,20},{28,24},{5,1},{9,5},{13... | collective-permute-start | bytes 196616 | tf_op jit(solution)/shard_map/ppermute | solution.py:21
  235.5 67.2 %collective-permute-start.14 = (f32[6,1,1024]{2,1,0:T(1,128)}, f32[6,1,1024]{2,1,0:T(1,128)}, u32[]{:S(2)}, u32[]{:S(2)}) collective-permute-start(f32[6,1,1024]{2,1,0:T(1,128)} %get-tuple-element.64), channel_id=1, source_target_pairs={{0,1},{1,2},{2,3},{4,5},{5,6},{6,7},{8,9},{9,10},{10,11},{12,13},{... | collective-permute-start | bytes 73736 | tf_op jit(solution)/shard_map/ppermute | solution.py:19
  237.3 65.4 %collective-permute-start.15 = (f32[6,1,1024]{2,1,0:T(1,128)}, f32[6,1,1024]{2,1,0:T(1,128)}, u32[]{:S(2)}, u32[]{:S(2)}) collective-permute-start(f32[6,1,1024]{2,1,0:T(1,128)} %get-tuple-element.65), channel_id=1, source_target_pairs={{1,0},{2,1},{3,2},{5,4},{6,5},{7,6},{9,8},{10,9},{11,10},{13,12},{... | collective-permute-start | bytes 73736 | tf_op jit(solution)/shard_map/ppermute | solution.py:21
  238.9 6.1 %collective-permute-start.34 = (f32[6,1,1024]{2,1,0:T(1,128)S(1)}, f32[6,1,1024]{2,1,0:T(1,128)S(1)}, u32[]{:S(2)}, u32[]{:S(2)}) collective-permute-start(f32[6,1,1024]{2,1,0:T(1,128)S(1)} %get-tuple-element.54), channel_id=1, source_target_pairs={{0,1},{1,2},{2,3},{4,5},{5,6},{6,7},{8,9},{9,10},{10,11},{12,13},{... | collective-permute-start | bytes 73736 | tf_op jit(solution)/shard_map/ppermute | solution.py:19
  296.8 7.9 %collective-permute-start.36 = (f32[1,16,1024]{2,1,0:T(8,128)S(1)}, f32[1,16,1024]{2,1,0:T(8,128)S(1)}, u32[]{:S(2)}, u32[]{:S(2)}) collective-permute-start(f32[1,16,1024]{2,1,0:T(8,128)S(1)} %get-tuple-element.74), channel_id=1, source_target_pairs={{0,4},{4,8},{8,12},{12,16},{16,20},{20,24},{24,28},{1,5},{5,9},{9,... | collective-permute-start | bytes 196616 | tf_op jit(solution)/shard_map/ppermute | solution.py:19
  301.4 6.2 %collective-permute-start.37 = (f32[1,16,1024]{2,1,0:T(8,128)S(1)}, f32[1,16,1024]{2,1,0:T(8,128)S(1)}, u32[]{:S(2)}, u32[]{:S(2)}) collective-permute-start(f32[1,16,1024]{2,1,0:T(8,128)S(1)} %get-tuple-element.75), channel_id=1, source_target_pairs={{4,0},{8,4},{12,8},{16,12},{20,16},{24,20},{28,24},{5,1},{9,5},{13... | collective-permute-start | bytes 196616 | tf_op jit(solution)/shard_map/ppermute | solution.py:21
  308.9 4.9 %collective-permute-start.39 = (f32[6,1,1024]{2,1,0:T(1,128)S(1)}, f32[6,1,1024]{2,1,0:T(1,128)S(1)}, u32[]{:S(2)}, u32[]{:S(2)}) collective-permute-start(f32[6,1,1024]{2,1,0:T(1,128)S(1)} %get-tuple-element.53), channel_id=1, source_target_pairs={{1,0},{2,1},{3,2},{5,4},{6,5},{7,6},{9,8},{10,9},{11,10},{13,12},{... | collective-permute-start | bytes 73736 | tf_op jit(solution)/shard_map/ppermute | solution.py:21
  (43 other events, 512.4 us)
where the time goes:
time: 363 us; the launch traced here: 361 us
  blocking collectives  183 us (50%)
  starting transfers between devices  96.6 us (27%)
  waiting for transfers between devices  38 us (10%)
  other arithmetic  19.5 us (5%)
  between operations  14.5 us (4%)
  local copies, waits for them, and re-layouts  8.88 us (2%)
    psum x4, blocking collectives, paired(): lax.psum((jnp.sum(residual_now * scaled_now), jnp.sum(scaled_now * image_...  166 us
    ppermute x20, starting transfers between devices, padded_2(): lax.ppermute(tail, axis, [(i, (i + 1) % count) for i in range(ends)])  70.2 us
    ppermute x20, waiting for transfers between devices, padded_2(): lax.ppermute(head, axis, [((i + 1) % count, i) for i in range(ends)])  37.1 us
    ppermute x20, starting transfers between devices, padded_2(): lax.ppermute(head, axis, [((i + 1) % count, i) for i in range(ends)])  26.3 us
  transfers between devices with their start and end apart: 40, of which 14 were waited for; matrix products, arithmetic and copies ran while one was open for 5% of the time, Pallas kernels for 0%

commit v1 on v0

v1 whole, which is shorter than its diff:
```python
import functools

import jax
import jax.numpy as jnp
from jax import lax
from jax.experimental import pallas as pl
from jax.experimental.pallas import tpu as pltpu
from jax.sharding import PartitionSpec as P

SUBSTEPS = 4
ITERS = 4
ZB = 128
LANES = 128
MESH = pl.DeviceIdType.MESH
F32 = jnp.float32

ST_P = 0
ST_U = ST_P + SUBSTEPS - 1
ST_K = ST_U + SUBSTEPS
ST_V = ST_K + 1
ST_W = ST_V + 1
STAGES = ST_W + ITERS


def kernel(
    nx, ny,
    u_hbm, d_hbm, c_hbm, flags_hbm, v_hbm, cap_hbm, k_hbm, heat_hbm, map_hbm,
    u_out, v_out,
    U, Pb, K, V, W,
    yU, yP, yK, yV, yW,
    sU, sP, sK, sV, sW,
    D, C, FLAGS, CAP, HEAT, MAP,
    CC, CXm, CXp, CYm, CYp, CZm, CZp, Q, GH, LK, FS,
    GX, GYm, GYp, GZm, GZp, DI, INV,
    TG, AG, MU, MGY, MSX, MGX, UO, VO,
    in_sem, out_sem, hs_sem, hr_sem, tg_s, tg_r, ag_s, ag_r, my_s, my_r, mx_s, mx_r,
):
    gx = lax.axis_index("gx")
    gy = lax.axis_index("gy")
    lx, ly, zz = CAP.shape
    wg = TG.shape[-1]

    loads = {}

    def load(name, src, dst, n):
        cp = pltpu.make_async_copy(src, dst, in_sem.at[n])
        cp.start()
        loads[name] = cp

    load("u", u_hbm, U.at[0, pl.ds(1, lx)], 0)
    load("v", v_hbm, V.at[pl.ds(1, lx)], 1)
    load("k", k_hbm, K.at[pl.ds(1, lx)], 2)
    load("map", map_hbm, MAP, 3)
    load("flags", flags_hbm, FLAGS, 4)
    load("d", d_hbm, D, 5)
    load("c", c_hbm, C, 6)
    load("heat", heat_hbm, HEAT, 7)
    load("cap", cap_hbm, CAP, 8)

    barrier = pltpu.get_barrier_semaphore()
    for p in range(1, nx):
        pl.semaphore_signal(barrier, 1, device_id={"gx": lax.rem(gx + p, nx)}, device_id_type=MESH)
    for p in range(1, ny):
        pl.semaphore_signal(barrier, 1, device_id={"gy": lax.rem(gy + p, ny)}, device_id_type=MESH)

    bodies = (
        [(Pb.at[s], yP.at[s]) for s in range(SUBSTEPS - 1)]
        + [(U.at[s], yU.at[s]) for s in range(SUBSTEPS)]
        + [(K, yK), (V, yV)]
        + [(W.at[s], yW.at[s]) for s in range(ITERS)]
    )
    stagings = (
        [sP.at[s] for s in range(SUBSTEPS - 1)]
        + [sU.at[s] for s in range(SUBSTEPS)]
        + [sK, sV]
        + [sW.at[s] for s in range(ITERS)]
    )

    @pl.when(gx == 0)
    def _():
        for body, _y in bodies:
            body[0] = jnp.zeros(body.shape[1:], F32)

    @pl.when(gx == nx - 1)
    def _():
        for body, _y in bodies:
            body[lx + 1] = jnp.zeros(body.shape[1:], F32)

    @pl.when(gy == 0)
    def _():
        for _b, y in bodies:
            y[0] = jnp.zeros(y.shape[1:], F32)

    @pl.when(gy == ny - 1)
    def _():
        for _b, y in bodies:
            y[1] = jnp.zeros(y.shape[1:], F32)

    pl.semaphore_wait(barrier, nx + ny - 2)

    has = (gx > 0, gx < nx - 1, gy > 0, gy < ny - 1)
    to = (
        {"gx": jnp.maximum(gx - 1, 0)},
        {"gx": jnp.minimum(gx + 1, nx - 1)},
        {"gy": jnp.maximum(gy - 1, 0)},
        {"gy": jnp.minimum(gy + 1, ny - 1)},
    )

    def halo_copy(stage, d):
        body, y = bodies[stage]
        stag = stagings[stage]
        src, dst = (
            (body.at[1], body.at[lx + 1]),
            (body.at[lx], body.at[0]),
            (stag.at[0], y.at[1]),
            (stag.at[1], y.at[0]),
        )[d]
        return pltpu.make_async_remote_copy(
            src_ref=src, dst_ref=dst, send_sem=hs_sem.at[stage, d], recv_sem=hr_sem.at[stage, d],
            device_id=to[d], device_id_type=MESH,
        )

    def send(stage):
        for d in (0, 1, 2, 3):
            @pl.when(has[d])
            def _():
                halo_copy(stage, d).start()

    def arrive(stage):
        for d in (0, 1, 2, 3):
            @pl.when(has[d ^ 1])
            def _():
                halo_copy(stage, d).wait_recv()

    def sent(stage):
        for d in (0, 1, 2, 3):
            @pl.when(has[d])
            def _():
                halo_copy(stage, d).wait_send()

    def gather(buf, axis, n, me, ss, rs):
        copies = []
        for p in range(1, n):
            cp = pltpu.make_async_remote_copy(
                src_ref=buf.at[0], dst_ref=buf.at[p], send_sem=ss.at[p], recv_sem=rs.at[p],
                device_id={axis: lax.rem(me + p, n)}, device_id_type=MESH,
            )
            cp.start()
            copies.append(cp)
        return copies

    def rows(fn):
        def step(i, carry):
            fn(i)
            return carry
        lax.fori_loop(0, lx, step, 0)

    def stage_y(stage, i, x):
        stag = stagings[stage]
        stag[0, i] = x[0:1, :]
        stag[1, i] = x[ly - 1:ly, :]

    def sides(body, y, i):
        x = body[i + 1]
        z = x.shape[1]
        sub = lax.broadcasted_iota(jnp.int32, x.shape, 0)
        ym = jnp.where(sub == 0, y[0, i], pltpu.roll(x, 1, 0))
        yp = jnp.where(sub == ly - 1, y[1, i], pltpu.roll(x, ly - 1, 0))
        return x, body[i], body[i + 2], ym, yp, pltpu.roll(x, 1, 1), pltpu.roll(x, z - 1, 1)

    lane_g = lax.broadcasted_iota(jnp.int32, (ly, wg), 1)
    sub_g = lax.broadcasted_iota(jnp.int32, (ly, wg), 0)
    own_g = lane_g == gy * ly + sub_g
    lane_gf = lane_g.astype(F32)
    lane_t = lax.broadcasted_iota(jnp.int32, (ly, LANES), 1)
    lane_z = lax.broadcasted_iota(jnp.int32, (ly, zz), 1)

    loads["u"].wait()

    def take_low(i):
        x = U[0, i + 1, :, 0:LANES]
        Pb[0, i + 1] = x
        stage_y(ST_P, i, x)
    rows(take_low)
    send(ST_P)

    loads["v"].wait()

    def take_top(i):
        last = V[i + 1, :, zz - LANES:zz]
        TG[0, i] = jnp.sum(jnp.where(own_g, last[:, LANES - 1:LANES], 0.0), axis=0, keepdims=True)
        stage_y(ST_V, i, V[i + 1])
        stage_y(ST_U, i, U[0, i + 1])
    rows(take_top)
    tops = gather(TG, "gy", ny, gy, tg_s, tg_r)

    loads["k"].wait()

    def take_k(i):
        stage_y(ST_K, i, K[i + 1])
    rows(take_k)
    send(ST_K)

    loads["map"].wait()
    loads["flags"].wait()
    loads["d"].wait()
    loads["c"].wait()
    eye = lax.broadcasted_iota(jnp.int32, (ly, ly), 0) == lax.broadcasted_iota(jnp.int32, (ly, ly), 1)
    for i in range(lx):
        line = MAP[i:i + 1, :].astype(F32)
        lk = jnp.sum(jnp.where(eye, line, 0.0), axis=1, keepdims=True)
        LK[i] = jnp.broadcast_to(lk, (ly, LANES))

    def fluid_coefficients(i):
        flags = FLAGS[i].astype(F32)
        for t in range(zz // ZB):
            sl = pl.ds(t * ZB, ZB)
            on = jnp.broadcast_to(flags[:, t:t + 1], (ly, ZB))
            spread = on * D[i, :, sl]
            total = None
            for comp, (lo, hi) in enumerate(((CXm, CXp), (CYm, CYp), (CZm, CZp))):
                flow = on * C[comp, i, :, sl]
                a = spread + jnp.maximum(flow, 0.0)
                b = spread - jnp.minimum(flow, 0.0)
                total = a + b if total is None else total + (a + b)
                if comp == 2 and t == 0:
                    lane = lax.broadcasted_iota(jnp.int32, (ly, ZB), 1)
                    Q[i] = jnp.where(lane == 0, a, 0.0)[:, 0:LANES]
                    a = jnp.where(lane == 0, 0.0, a)
                if comp == 2 and t == zz // ZB - 1:
                    lane = lax.broadcasted_iota(jnp.int32, (ly, ZB), 1)
                    b = jnp.where(lane == ZB - 1, 0.0, b)
                lo[i, :, sl] = a
                hi[i, :, sl] = b
            CC[i, :, sl] = 1.0 - total
    rows(fluid_coefficients)

    for cp in tops:
        cp.wait_recv()

    def ghosts(i):
        whole = TG[0, i]
        for p in range(1, ny):
            whole = whole + TG[p, i]
        pick = jnp.where(lane_gf == LK[i, :, 0:1], whole, 0.0)
        ghost = jnp.sum(pick, axis=1, keepdims=True)
        GH[i] = jnp.broadcast_to(ghost, (ly, LANES))
        Q[i] = Q[i] * ghost
        FS[i] = Pb[0, i + 1] - ghost
    rows(ghosts)

    def fluid(body, y, i, z):
        x, a, b, c, d, e, f = sides(body, y, i)
        sl = pl.ds(0, z)
        return (CC[i, :, sl] * x + CXm[i, :, sl] * a + CXp[i, :, sl] * b + CYm[i, :, sl] * c
                + CYp[i, :, sl] * d + CZm[i, :, sl] * e + CZp[i, :, sl] * f)

    for s in range(SUBSTEPS - 1):
        arrive(ST_P + s)

        def low(i):
            new = fluid(Pb.at[s], yP.at[s], i, LANES) + Q[i]
            FS[i] = FS[i] + (new - GH[i])
            if s + 1 < SUBSTEPS - 1:
                Pb[s + 1, i + 1] = new
                stage_y(ST_P + s + 1, i, new)
        rows(low)
        if s + 1 < SUBSTEPS - 1:
            send(ST_P + s + 1)
        if s == 0:
            send(ST_V)

    def scatter(i):
        mean = FS[i][:, 0:1] * (1.0 / SUBSTEPS)
        AG[0, i] = jnp.sum(jnp.where(lane_gf == LK[i, :, 0:1], mean, 0.0), axis=0, keepdims=True)
    rows(scatter)
    fluxes = gather(AG, "gy", ny, gy, ag_s, ag_r)
    send(ST_U)

    arrive(ST_K)
    loads["cap"].wait()
    loads["heat"].wait()
    for f in range(lx + 1):
        GX[f] = 0.5 * (K[f] + K[f + 1])

    def solid_coefficients(i):
        k, _a, _b, c, d, e, f = sides(K, yK, i)
        gxm, gxp, gym, gyp = GX[i], GX[i + 1], 0.5 * (k + c), 0.5 * (k + d)
        gzm = 0.5 * (k + jnp.where(lane_z == 0, 0.0, e))
        gzp = 0.5 * (k + jnp.where(lane_z == zz - 1, 0.0, f))
        diag = CAP[i] + (gxm + gxp + gym + gyp + gzm + gzp)
        DI[i] = diag
        INV[i] = 1.0 / diag
        GYm[i] = gym
        GYp[i] = gyp
        GZm[i] = jnp.where(lane_z == 0, 0.0, gzm)
        GZp[i] = jnp.where(lane_z == zz - 1, 0.0, gzp)
    rows(solid_coefficients)

    def pull(body, y, i):
        x, a, b, c, d, e, f = sides(body, y, i)
        return x, (GX[i] * a + GX[i + 1] * b + GYm[i] * c + GYp[i] * d + GZm[i] * e + GZp[i] * f)

    arrive(ST_V)

    def first(i):
        x, s = pull(V, yV, i)
        W[0, i + 1] = (HEAT[i] - (DI[i] - CAP[i]) * x + s) * INV[i]
    rows(first)

    for cp in fluxes:
        cp.wait_recv()

    def fold(x):
        acc = x[0:8, 0:LANES]
        for r in range(0, ly, 8):
            for t in range(0, zz, LANES):
                if r or t:
                    acc = acc + x[r:r + 8, t:t + LANES]
        return jnp.sum(acc, axis=0, keepdims=True)

    def add_flux(i):
        whole = AG[0, i]
        for p in range(1, ny):
            whole = whole + AG[p, i]
        got = jnp.sum(jnp.where(own_g, whole, 0.0), axis=1, keepdims=True)
        sl = pl.ds(zz - LANES, LANES)
        W[0, i + 1, :, sl] = W[0, i + 1, :, sl] + jnp.where(lane_t == LANES - 1, got, 0.0) * INV[i, :, sl]
        stage_y(ST_W, i, W[0, i + 1])
    rows(add_flux)
    send(ST_W)

    MU[...] = jnp.zeros(MU.shape, F32)

    def norm(i):
        w = W[0, i + 1]
        MU[0:1] = MU[0:1] + fold(w * w * DI[i])
    rows(norm)

    for s in range(max(SUBSTEPS, ITERS)):
        if s < SUBSTEPS:
            arrive(ST_U + s)
            last_u = s + 1 == SUBSTEPS

            def bulk(i):
                new = fluid(U.at[s], yU.at[s], i, zz)
                head = new[:, 0:LANES] + Q[i]
                if last_u:
                    UO[i] = new
                    UO[i, :, 0:LANES] = head
                else:
                    U[s + 1, i + 1] = new
                    U[s + 1, i + 1, :, 0:LANES] = head
                    stage_y(ST_U + s + 1, i, U[s + 1, i + 1])
            rows(bulk)
            if last_u:
                out_u = pltpu.make_async_copy(UO, u_out, out_sem.at[0])
                out_u.start()
            else:
                send(ST_U + s + 1)
        if s < ITERS:
            arrive(ST_W + s)
            last_w = s + 1 == ITERS

            def apply(i):
                x, pulled = pull(W.at[s], yW.at[s], i)
                MU[2 * s + 1:2 * s + 2] = MU[2 * s + 1:2 * s + 2] + fold(x * pulled)
                if not last_w:
                    new = pulled * INV[i]
                    W[s + 1, i + 1] = new
                    stage_y(ST_W + s + 1, i, new)
                    MU[2 * s + 2:2 * s + 3] = MU[2 * s + 2:2 * s + 3] + fold(new * pulled)
            rows(apply)
            if not last_w:
                send(ST_W + s + 1)

    MGY[0] = MU[...]
    sums_y = gather(MGY, "gy", ny, gy, my_s, my_r)
    for cp in sums_y:
        cp.wait_recv()
    total = MGY[0]
    for p in range(1, ny):
        total = total + MGY[p]
    MGX[0] = jnp.broadcast_to(jnp.sum(total, axis=1, keepdims=True), total.shape)
    sums_x = gather(MGX, "gx", nx, gx, mx_s, mx_r)
    for cp in sums_x:
        cp.wait_recv()


    total = jnp.zeros(MU.shape, F32)
    for p in range(nx):
        total = total + MGX[p]
    mu = [total[m:m + 1, :] for m in range(2 * ITERS)]

    tiny = 1e-30
    G = [[mu[i + j] - mu[i + j + 1] for j in range(ITERS)] for i in range(ITERS)]
    b = [mu[i] for i in range(ITERS)]
    low_f = {}
    rec = []
    for i in range(ITERS):
        good = G[i][i] > jnp.maximum(1e-7 * (mu[2 * i] + jnp.abs(mu[2 * i + 1])), tiny)
        r = jnp.where(good, 1.0 / jnp.where(good, G[i][i], 1.0), 0.0)
        rec.append(r)
        for j in range(i + 1, ITERS):
            low_f[j, i] = G[j][i] * r
        for j in range(i + 1, ITERS):
            b[j] = b[j] - low_f[j, i] * b[i]
            for m in range(i + 1, ITERS):
                G[j][m] = G[j][m] - low_f[j, i] * G[i][m]
    y = [None] * ITERS
    for i in reversed(range(ITERS)):
        y[i] = b[i] * rec[i]
        for j in range(i + 1, ITERS):
            y[i] = y[i] - low_f[j, i] * y[j]

    ys = [v[:, 0:1] for v in y]

    def finish(i):
        acc = V[i + 1]
        for j in range(ITERS):
            acc = acc + ys[j] * W[j, i + 1]
        VO[i] = acc
    rows(finish)
    out_v = pltpu.make_async_copy(VO, v_out, out_sem.at[1])
    out_v.start()

    for stage in range(STAGES):
        sent(stage)
    for cp in tops + fluxes + sums_y + sums_x:
        cp.wait_send()
    out_u.wait()
    out_v.wait()


def solution(mesh):
    nx, ny = mesh.shape["gx"], mesh.shape["gy"]

    def local(u, d, c, flags, v, cap, k, heat, lookup):
        lx, ly, zz = u.shape
        wg = -(-(ny * ly) // LANES) * LANES
        field = (lx, ly, zz)
        padded = (lx + 2, ly, zz)
        edge = (2, lx, 1, zz)
        low = (2, lx, 1, LANES)
        tile = (lx, ly, LANES)
        vm = lambda *shape: pltpu.VMEM(shape, F32)
        ns = SUBSTEPS
        scratch = [
            vm(ns, *padded), vm(ns - 1, lx + 2, ly, LANES), vm(*padded), vm(*padded), vm(ITERS, *padded),
            vm(ns, *edge), vm(ns - 1, *low), vm(*edge), vm(*edge), vm(ITERS, *edge),
            vm(ns, *edge), vm(ns - 1, *low), vm(*edge), vm(*edge), vm(ITERS, *edge),
            vm(*field), vm(3, *field), pltpu.VMEM(flags.shape, jnp.int32), vm(*field), vm(*field),
            pltpu.VMEM(lookup.shape, jnp.int32),
        ]
        scratch += [vm(*field)] * 7 + [vm(*tile)] * 4
        scratch += [vm(lx + 1, ly, zz)] + [vm(*field)] * 6
        scratch += [
            vm(ny, lx, 1, wg), vm(ny, lx, 1, wg), vm(2 * ITERS, LANES), vm(ny, 2 * ITERS, LANES),
            vm(2 * ITERS, LANES), vm(nx, 2 * ITERS, LANES), vm(*field), vm(*field),
        ]
        dma = lambda *shape: pltpu.SemaphoreType.DMA(shape)
        scratch += [
            dma(9), dma(2), dma(STAGES, 4), dma(STAGES, 4),
            dma(ny), dma(ny), dma(ny), dma(ny), dma(ny), dma(ny), dma(nx), dma(nx),
        ]
        return pl.pallas_call(
            functools.partial(kernel, nx, ny),
            out_shape=(jax.ShapeDtypeStruct(field, F32),) * 2,
            in_specs=[pl.BlockSpec(memory_space=pl.ANY)] * 9,
            out_specs=(pl.BlockSpec(memory_space=pl.ANY),) * 2,
            scratch_shapes=scratch,
            compiler_params=pltpu.CompilerParams(
                collective_id=0, has_side_effects=True, vmem_limit_bytes=40 * 1024 * 1024
            ),
        )(u, d, c, flags, v, cap, k, heat, lookup)

    s3 = P("gx", "gy", None)
    return jax.shard_map(
        local,
        mesh=mesh,
        in_specs=(s3, s3, P(None, "gx", "gy", None), s3, s3, s3, s3, s3, P("gx", "gy")),
        out_specs=(s3, s3),
        check_vma=False,
    )
```

time: 363 us -> 63.8 us (0.18)
  blocking collectives: 183 us -> 0 us
  starting transfers between devices: 96.6 us -> 0 us
  Pallas kernels: 0 us -> 53.7 us
  waiting for transfers between devices: 38 us -> 0 us
  other arithmetic: 19.5 us -> 0 us
  between operations: 14.5 us -> 0.65 us
    psum x4 -> x0, blocking collectives: 166 us -> none  [paired(): lax.psum((jnp.sum(residual_now * scaled_now), jnp.sum(scaled_now * image_...]
    ppermute x40 -> x0, starting transfers between devices: 96.6 us -> none  [the longest x20 70.2 us: padded_2(): lax.ppermute(tail, axis, [(i, (i + 1) % count) for i in range(ends)])]
    pallas_call x0 -> x1, Pallas kernels: none -> 53.7 us  [local(): pl.pallas_call(functools.partial(kernel, nx, ny), out_shape=(jax.ShapeDty...]
    ppermute x40 -> x0, waiting for transfers between devices: 38 us -> none  [the longest x20 37.1 us: padded_2(): lax.ppermute(head, axis, [((i + 1) % count, i) for i in range(ends)])]
    all_gather x3 -> x0, blocking collectives: 17.4 us -> none  [the longest x1 6.64 us: local(): flux_wide = lax.all_gather(flux_mean, 'gy', axis=1, tiled=True)]
    reduce_sum x7 -> x0, other arithmetic: 8.37 us -> none  [the longest x4 6.04 us: paired(): jnp.sum(scaled_now * image_now)]
    unnamed x77 -> x19, local copies, waits for them, and re-layouts: 2.28 us -> 9.04 us
    slice x28 -> x0, local copies, waits for them, and re-layouts: 5.77 us -> none  [the longest x11 1.75 us: padded_2(): lax.slice_in_dim(cells, cells.shape[dim] - width, cells.shape[dim], axis=...]
  transfers between devices with their start and end apart: 40 -> 0, of which waited for: 14 -> 0; matrix products, arithmetic and copies ran while one was open for 5% -> 0% of each run, Pallas kernels for 0% -> 0%
where the time goes in v1:
time: 63.8 us; the launch traced here: 63.4 us
  Pallas kernels  53.7 us (84%)
  local copies, waits for them, and re-layouts  9.04 us (14%)
  between operations  0.65 us (1%)
    pallas_call x1, Pallas kernels, local(): pl.pallas_call(functools.partial(kernel, nx, ny), out_shape=(jax.ShapeDty...  53.7 us
    unnamed x19, local copies, waits for them, and re-layouts  9.04 us

profile of v1, /device:TPU:0, one launch (start us, length us, event | category | flops | bytes accessed | tf_op | source)
XLA Modules:
  0.0 63.4 jit_solution(16500258924769246803)
XLA Ops:
  0.6 0.0 copy-start.7
  0.6 0.8 %copy.11.flags_hbm = s32[4,16,8]{2,1,0:T(8,128)S(1)} copy(s32[4,16,8]{1,2,0:T(8,128)} %param.12) | data formatting | bytes 4096 | tf_op args[3]
  1.4 0.0 copy-done.7
  1.4 0.0 copy-start
  1.4 1.1 %copy-done = f32[3,4,16,1024]{3,2,1,0:T(8,128)S(1)} copy-done((f32[3,4,16,1024]{3,2,1,0:T(8,128)S(1)}, f32[3,4,16,1024]{3,2,1,0:T(8,128)}, u32[]{:S(2)}) %copy-start) | copy-done | bytes 786456
  2.6 0.0 copy-start.1
  2.6 0.9 %copy-done.1 = f32[4,16,1024]{2,1,0:T(8,128)S(1)} copy-done((f32[4,16,1024]{2,1,0:T(8,128)S(1)}, f32[4,16,1024]{2,1,0:T(8,128)}, u32[]{:S(2)}) %copy-start.1) | copy-done | bytes 262168
  3.5 0.0 copy-start.2
  3.5 0.9 %copy-done.2 = f32[4,16,1024]{2,1,0:T(8,128)S(1)} copy-done((f32[4,16,1024]{2,1,0:T(8,128)S(1)}, f32[4,16,1024]{2,1,0:T(8,128)}, u32[]{:S(2)}) %copy-start.2) | copy-done | bytes 262168
  4.5 0.0 copy-start.3
  4.5 0.9 %copy-done.3 = f32[4,16,1024]{2,1,0:T(8,128)S(1)} copy-done((f32[4,16,1024]{2,1,0:T(8,128)S(1)}, f32[4,16,1024]{2,1,0:T(8,128)}, u32[]{:S(2)}) %copy-start.3) | copy-done | bytes 262168
  5.4 0.0 copy-start.4
  5.4 0.9 %copy-done.4 = f32[4,16,1024]{2,1,0:T(8,128)S(1)} copy-done((f32[4,16,1024]{2,1,0:T(8,128)S(1)}, f32[4,16,1024]{2,1,0:T(8,128)}, u32[]{:S(2)}) %copy-start.4) | copy-done | bytes 262168
  6.4 0.0 copy-start.5
  6.4 0.9 %copy-done.5 = f32[4,16,1024]{2,1,0:T(8,128)S(1)} copy-done((f32[4,16,1024]{2,1,0:T(8,128)S(1)}, f32[4,16,1024]{2,1,0:T(8,128)}, u32[]{:S(2)}) %copy-start.5) | copy-done | bytes 262168
  7.3 0.0 copy-start.6
  7.3 0.9 %copy-done.6 = f32[4,16,1024]{2,1,0:T(8,128)S(1)} copy-done((f32[4,16,1024]{2,1,0:T(8,128)S(1)}, f32[4,16,1024]{2,1,0:T(8,128)}, u32[]{:S(2)}) %copy-start.6) | copy-done | bytes 262168
  8.3 53.7 %shard_map.104 = (f32[4,16,1024]{2,1,0:T(8,128)S(1)}, f32[4,16,1024]{2,1,0:T(8,128)S(1)}) custom-call(f32[4,16,1024]{2,1,0:T(8,128)S(1)} %copy-done.1, f32[4,16,1024]{2,1,0:T(8,128)S(1)} %copy-done.2, f32[3,4,16,1024]{3,2,1,0:T(8,128)S(1)} %copy-done, s32[4,16,8]{2,1,0:T(8,128)S(1)} %copy.11.flags_hbm, f32[4,16,1024]{2,1,0:T(8,128)S(1)} %copy-done.3, ...), custom_call_target="tpu_custom_call" | custom-call | tf_op jit(solution)/shard_map/pallas_call | solution.py:466
  62.0 0.7 %copy.14 = f32[4,16,1024]{2,1,0:T(8,128)} copy(f32[4,16,1024]{2,1,0:T(8,128)S(1)} %get-tuple-element.4) | data formatting | bytes 524288
  62.7 0.7 %copy.15 = f32[4,16,1024]{2,1,0:T(8,128)} copy(f32[4,16,1024]{2,1,0:T(8,128)S(1)} %get-tuple-element.5) | data formatting | bytes 524288
Async XLA Ops:
  0.6 0.8 %copy-start.7 = (s32[4,16]{1,0:T(4,128)S(1)}, s32[4,16]{1,0:T(4,128)}, u32[]{:S(2)}) copy-start(s32[4,16]{1,0:T(4,128)} %map_hbm.1) | copy-start | bytes 772
  1.4 1.1 %copy-start = (f32[3,4,16,1024]{3,2,1,0:T(8,128)S(1)}, f32[3,4,16,1024]{3,2,1,0:T(8,128)}, u32[]{:S(2)}) copy-start(f32[3,4,16,1024]{3,2,1,0:T(8,128)} %c_hbm.1) | copy-start | bytes 2359300
  2.6 0.9 %copy-start.1 = (f32[4,16,1024]{2,1,0:T(8,128)S(1)}, f32[4,16,1024]{2,1,0:T(8,128)}, u32[]{:S(2)}) copy-start(f32[4,16,1024]{2,1,0:T(8,128)} %u_hbm.1) | copy-start | bytes 786436
  3.5 0.9 %copy-start.2 = (f32[4,16,1024]{2,1,0:T(8,128)S(1)}, f32[4,16,1024]{2,1,0:T(8,128)}, u32[]{:S(2)}) copy-start(f32[4,16,1024]{2,1,0:T(8,128)} %d_hbm.1) | copy-start | bytes 786436
  4.5 0.9 %copy-start.3 = (f32[4,16,1024]{2,1,0:T(8,128)S(1)}, f32[4,16,1024]{2,1,0:T(8,128)}, u32[]{:S(2)}) copy-start(f32[4,16,1024]{2,1,0:T(8,128)} %v_hbm.1) | copy-start | bytes 786436
  5.4 0.9 %copy-start.4 = (f32[4,16,1024]{2,1,0:T(8,128)S(1)}, f32[4,16,1024]{2,1,0:T(8,128)}, u32[]{:S(2)}) copy-start(f32[4,16,1024]{2,1,0:T(8,128)} %cap_hbm.1) | copy-start | bytes 786436
  6.4 0.9 %copy-start.5 = (f32[4,16,1024]{2,1,0:T(8,128)S(1)}, f32[4,16,1024]{2,1,0:T(8,128)}, u32[]{:S(2)}) copy-start(f32[4,16,1024]{2,1,0:T(8,128)} %k_hbm.1) | copy-start | bytes 786436
  7.3 0.9 %copy-start.6 = (f32[4,16,1024]{2,1,0:T(8,128)S(1)}, f32[4,16,1024]{2,1,0:T(8,128)}, u32[]{:S(2)}) copy-start(f32[4,16,1024]{2,1,0:T(8,128)} %heat_hbm.1) | copy-start | bytes 786436

commit v2 on v1

--- a/solution.py
+++ b/solution.py
@@ -96,6 +96,8 @@
         for _b, y in bodies:
             y[1] = jnp.zeros(y.shape[1:], F32)
 
+    W[ITERS - 1, lx + 1] = jnp.zeros((ly, zz), F32)
+
     pl.semaphore_wait(barrier, nx + ny - 2)
 
     has = (gx > 0, gx < nx - 1, gy > 0, gy < ny - 1)
@@ -120,20 +122,25 @@
             device_id=to[d], device_id_type=MESH,
         )
 
-    def send(stage):
-        for d in (0, 1, 2, 3):
+    one_way = ST_W + ITERS - 1
+
+    def dirs(stage, among=(0, 1, 2, 3)):
+        return [d for d in among if stage != one_way or d in (1, 3)]
+
+    def send(stage, among=(0, 1, 2, 3)):
+        for d in dirs(stage, among):
             @pl.when(has[d])
             def _():
                 halo_copy(stage, d).start()
 
     def arrive(stage):
-        for d in (0, 1, 2, 3):
+        for d in dirs(stage):
             @pl.when(has[d ^ 1])
             def _():
                 halo_copy(stage, d).wait_recv()
 
     def sent(stage):
-        for d in (0, 1, 2, 3):
+        for d in dirs(stage):
             @pl.when(has[d])
             def _():
                 halo_copy(stage, d).wait_send()
@@ -149,11 +156,17 @@
             copies.append(cp)
         return copies
 
-    def rows(fn):
-        def step(i, carry):
-            fn(i)
+    def rows(fn, stage=None):
+        def step(t, carry):
+            fn(lax.rem(lx - t, lx))
+            if stage is not None:
+                @pl.when(t == min(1, lx - 1))
+                def _():
+                    send(stage, (0, 1))
             return carry
         lax.fori_loop(0, lx, step, 0)
+        if stage is not None:
+            send(stage, (2, 3))
 
     def stage_y(stage, i, x):
         stag = stagings[stage]
@@ -181,8 +194,7 @@
         x = U[0, i + 1, :, 0:LANES]
         Pb[0, i + 1] = x
         stage_y(ST_P, i, x)
-    rows(take_low)
-    send(ST_P)
+    rows(take_low, ST_P)
 
     loads["v"].wait()
 
@@ -198,8 +210,7 @@
 
     def take_k(i):
         stage_y(ST_K, i, K[i + 1])
-    rows(take_k)
-    send(ST_K)
+    rows(take_k, ST_K)
 
     loads["map"].wait()
     loads["flags"].wait()
@@ -212,10 +223,10 @@
         LK[i] = jnp.broadcast_to(lk, (ly, LANES))
 
     def fluid_coefficients(i):
-        flags = FLAGS[i].astype(F32)
         for t in range(zz // ZB):
             sl = pl.ds(t * ZB, ZB)
-            on = jnp.broadcast_to(flags[:, t:t + 1], (ly, ZB))
+            line = FLAGS[i, t:t + 1, :].astype(F32)
+            on = jnp.broadcast_to(jnp.sum(jnp.where(eye, line, 0.0), axis=1, keepdims=True), (ly, ZB))
             spread = on * D[i, :, sl]
             total = None
             for comp, (lo, hi) in enumerate(((CXm, CXp), (CYm, CYp), (CZm, CZp))):
@@ -264,9 +275,7 @@
             if s + 1 < SUBSTEPS - 1:
                 Pb[s + 1, i + 1] = new
                 stage_y(ST_P + s + 1, i, new)
-        rows(low)
-        if s + 1 < SUBSTEPS - 1:
-            send(ST_P + s + 1)
+        rows(low, ST_P + s + 1 if s + 1 < SUBSTEPS - 1 else None)
         if s == 0:
             send(ST_V)
 
@@ -327,8 +336,7 @@
         sl = pl.ds(zz - LANES, LANES)
         W[0, i + 1, :, sl] = W[0, i + 1, :, sl] + jnp.where(lane_t == LANES - 1, got, 0.0) * INV[i, :, sl]
         stage_y(ST_W, i, W[0, i + 1])
-    rows(add_flux)
-    send(ST_W)
+    rows(add_flux, ST_W)
 
     MU[...] = jnp.zeros(MU.shape, F32)
 
@@ -337,42 +345,54 @@
         MU[0:1] = MU[0:1] + fold(w * w * DI[i])
     rows(norm)
 
-    for s in range(max(SUBSTEPS, ITERS)):
-        if s < SUBSTEPS:
-            arrive(ST_U + s)
-            last_u = s + 1 == SUBSTEPS
-
-            def bulk(i):
-                new = fluid(U.at[s], yU.at[s], i, zz)
-                head = new[:, 0:LANES] + Q[i]
-                if last_u:
-                    UO[i] = new
-                    UO[i, :, 0:LANES] = head
-                else:
-                    U[s + 1, i + 1] = new
-                    U[s + 1, i + 1, :, 0:LANES] = head
-                    stage_y(ST_U + s + 1, i, U[s + 1, i + 1])
-            rows(bulk)
+    def fluid_step(s):
+        arrive(ST_U + s)
+        last_u = s + 1 == SUBSTEPS
+
+        def bulk(i):
+            new = fluid(U.at[s], yU.at[s], i, zz)
+            head = new[:, 0:LANES] + Q[i]
             if last_u:
-                out_u = pltpu.make_async_copy(UO, u_out, out_sem.at[0])
-                out_u.start()
+                UO[i] = new
+                UO[i, :, 0:LANES] = head
             else:
-                send(ST_U + s + 1)
-        if s < ITERS:
-            arrive(ST_W + s)
-            last_w = s + 1 == ITERS
-
-            def apply(i):
-                x, pulled = pull(W.at[s], yW.at[s], i)
-                MU[2 * s + 1:2 * s + 2] = MU[2 * s + 1:2 * s + 2] + fold(x * pulled)
-                if not last_w:
-                    new = pulled * INV[i]
-                    W[s + 1, i + 1] = new
-                    stage_y(ST_W + s + 1, i, new)
-                    MU[2 * s + 2:2 * s + 3] = MU[2 * s + 2:2 * s + 3] + fold(new * pulled)
-            rows(apply)
-            if not last_w:
-                send(ST_W + s + 1)
+                U[s + 1, i + 1] = new
+                U[s + 1, i + 1, :, 0:LANES] = head
+                stage_y(ST_U + s + 1, i, U[s + 1, i + 1])
+        rows(bulk, None if last_u else ST_U + s + 1)
+
+    def solid_step(s):
+        arrive(ST_W + s)
+
+        def apply(i):
+            x, pulled = pull(W.at[s], yW.at[s], i)
+            MU[2 * s + 1:2 * s + 2] = MU[2 * s + 1:2 * s + 2] + fold(x * pulled)
+            new = pulled * INV[i]
+            W[s + 1, i + 1] = new
+            stage_y(ST_W + s + 1, i, new)
+            MU[2 * s + 2:2 * s + 3] = MU[2 * s + 2:2 * s + 3] + fold(new * pulled)
+        rows(apply, ST_W + s + 1)
+
+    for s in range(max(SUBSTEPS, ITERS) - 1):
+        if s < ITERS - 1:
+            solid_step(s)
+        if s < SUBSTEPS - 1:
+            fluid_step(s)
+
+    arrive(one_way)
+    end = ITERS - 1
+
+    def last_moment(i):
+        x = W[end, i + 1]
+        z = x.shape[1]
+        sub = lax.broadcasted_iota(jnp.int32, x.shape, 0)
+        twice = jnp.where(i == 0, 2.0, 1.0).astype(F32)
+        ym = jnp.where(sub == 0, 2.0 * yW[end, 0, i], pltpu.roll(x, 1, 0))
+        yp = jnp.where(sub == ly - 1, 0.0, pltpu.roll(x, ly - 1, 0))
+        pulled = (GX[i] * (twice * W[end, i]) + GX[i + 1] * W[end, i + 2] + GYm[i] * ym + GYp[i] * yp
+                  + GZm[i] * pltpu.roll(x, 1, 1) + GZp[i] * pltpu.roll(x, z - 1, 1))
+        MU[2 * end + 1:2 * end + 2] = MU[2 * end + 1:2 * end + 2] + fold(x * pulled)
+    rows(last_moment)
 
     MGY[0] = MU[...]
     sums_y = gather(MGY, "gy", ny, gy, my_s, my_r)
@@ -383,12 +403,13 @@
         total = total + MGY[p]
     MGX[0] = jnp.broadcast_to(jnp.sum(total, axis=1, keepdims=True), total.shape)
     sums_x = gather(MGX, "gx", nx, gx, mx_s, mx_r)
+    fluid_step(SUBSTEPS - 1)
+    out_u = pltpu.make_async_copy(UO, u_out, out_sem.at[0])
+    out_u.start()
     for cp in sums_x:
         cp.wait_recv()
-
-
-    total = jnp.zeros(MU.shape, F32)
-    for p in range(nx):
+    total = MGX[0]
+    for p in range(1, nx):
         total = total + MGX[p]
     mu = [total[m:m + 1, :] for m in range(2 * ITERS)]
 
@@ -449,7 +470,7 @@
             vm(ns, *padded), vm(ns - 1, lx + 2, ly, LANES), vm(*padded), vm(*padded), vm(ITERS, *padded),
             vm(ns, *edge), vm(ns - 1, *low), vm(*edge), vm(*edge), vm(ITERS, *edge),
             vm(ns, *edge), vm(ns - 1, *low), vm(*edge), vm(*edge), vm(ITERS, *edge),
-            vm(*field), vm(3, *field), pltpu.VMEM(flags.shape, jnp.int32), vm(*field), vm(*field),
+            vm(*field), vm(3, *field), pltpu.VMEM((lx, flags.shape[2], ly), jnp.int32), vm(*field), vm(*field),
             pltpu.VMEM(lookup.shape, jnp.int32),
         ]
         scratch += [vm(*field)] * 7 + [vm(*tile)] * 4
@@ -466,13 +487,13 @@
         return pl.pallas_call(
             functools.partial(kernel, nx, ny),
             out_shape=(jax.ShapeDtypeStruct(field, F32),) * 2,
-            in_specs=[pl.BlockSpec(memory_space=pl.ANY)] * 9,
+            in_specs=[pl.BlockSpec(memory_space=pltpu.HBM)] * 9,
             out_specs=(pl.BlockSpec(memory_space=pl.ANY),) * 2,
             scratch_shapes=scratch,
             compiler_params=pltpu.CompilerParams(
-                collective_id=0, has_side_effects=True, vmem_limit_bytes=40 * 1024 * 1024
+                collective_id=0, has_side_effects=True, vmem_limit_bytes=67_000_000
             ),
-        )(u, d, c, flags, v, cap, k, heat, lookup)
+        )(u, d, c, jnp.swapaxes(flags, 1, 2), v, cap, k, heat, lookup)
 
     s3 = P("gx", "gy", None)
     return jax.shard_map(

time: 63.8 us -> 55.1 us (0.86)
  local copies, waits for them, and re-layouts: 9.04 us -> 2.42 us
  Pallas kernels: 53.7 us -> 51.9 us
    unnamed x19 -> x4, local copies, waits for them, and re-layouts: 9.04 us -> 2.42 us
    pallas_call x1, Pallas kernels: 53.7 us -> 51.9 us  [local(): pl.pallas_call(functools.partial(kernel, nx, ny), out_shape=(jax.ShapeDty...]
where the time goes in v2:
time: 55.1 us; the launch traced here: 55 us
  Pallas kernels  51.9 us (94%)
  local copies, waits for them, and re-layouts  2.42 us (4%)
  between operations  0.65 us (1%)
    pallas_call x1, Pallas kernels, local(): pl.pallas_call(functools.partial(kernel, nx, ny), out_shape=(jax.ShapeDty...  51.9 us
    unnamed x4, local copies, waits for them, and re-layouts  2.42 us

profile of v2, /device:TPU:0, one launch (start us, length us, event | category | flops | bytes accessed | tf_op | source)
XLA Modules:
  0.0 55.0 jit_solution(9410316435098092128)
XLA Ops:
  0.6 51.9 %shard_map.104 = (f32[4,16,1024]{2,1,0:T(8,128)}, f32[4,16,1024]{2,1,0:T(8,128)}) custom-call(f32[4,16,1024]{2,1,0:T(8,128)} %u_hbm.1, f32[4,16,1024]{2,1,0:T(8,128)} %d_hbm.1, f32[3,4,16,1024]{3,2,1,0:T(8,128)} %c_hbm.1, s32[4,8,16]{2,1,0:T(8,128)} %bitcast.1, f32[4,16,1024]{2,1,0:T(8,128)} %v_hbm.1, f32[4,16,1024]{2,1,0:T(8,128)} %cap_hbm.1, ...), custom_call_target="tpu_custom_call" | custom-call | tf_op jit(solution)/shard_map/pallas_call | solution.py:487
  52.5 0.0 copy-start
  52.6 1.7 %copy.13 = f32[4,16,1024]{2,1,0:T(8,128)} copy(f32[4,16,1024]{2,1,0:T(8,128)} %get-tuple-element.4) | data formatting | bytes 524288
  54.3 0.0 copy-done
  54.3 0.7 %copy.14 = f32[4,16,1024]{2,1,0:T(8,128)} copy(f32[4,16,1024]{2,1,0:T(8,128)S(1)} %copy-done) | data formatting | bytes 524288
Async XLA Ops:
  52.5 1.7 %copy-start = (f32[4,16,1024]{2,1,0:T(8,128)S(1)}, f32[4,16,1024]{2,1,0:T(8,128)}, u32[]{:S(2)}) copy-start(f32[4,16,1024]{2,1,0:T(8,128)} %get-tuple-element.5) | copy-start | bytes 786436

commit v3 on v2

--- a/solution.py
+++ b/solution.py
@@ -20,6 +20,7 @@
 ST_V = ST_K + 1
 ST_W = ST_V + 1
 STAGES = ST_W + ITERS
+REACH = 1 + (SUBSTEPS - 1) + (ITERS - 1)
 
 
 def kernel(
@@ -58,8 +59,18 @@
     load("cap", cap_hbm, CAP, 8)
 
     barrier = pltpu.get_barrier_semaphore()
-    for p in range(1, nx):
-        pl.semaphore_signal(barrier, 1, device_id={"gx": lax.rem(gx + p, nx)}, device_id_type=MESH)
+    near = nx - 1 <= REACH
+    if near:
+        @pl.when(gx > 0)
+        def _():
+            pl.semaphore_signal(barrier, 1, device_id={"gx": jnp.maximum(gx - 1, 0)}, device_id_type=MESH)
+
+        @pl.when(gx < nx - 1)
+        def _():
+            pl.semaphore_signal(barrier, 1, device_id={"gx": jnp.minimum(gx + 1, nx - 1)}, device_id_type=MESH)
+    else:
+        for p in range(1, nx):
+            pl.semaphore_signal(barrier, 1, device_id={"gx": lax.rem(gx + p, nx)}, device_id_type=MESH)
     for p in range(1, ny):
         pl.semaphore_signal(barrier, 1, device_id={"gy": lax.rem(gy + p, ny)}, device_id_type=MESH)
 
@@ -98,7 +109,10 @@
 
     W[ITERS - 1, lx + 1] = jnp.zeros((ly, zz), F32)
 
-    pl.semaphore_wait(barrier, nx + ny - 2)
+    if near:
+        pl.semaphore_wait(barrier, ny + 1 - (gx == 0).astype(jnp.int32) - (gx == nx - 1).astype(jnp.int32))
+    else:
+        pl.semaphore_wait(barrier, nx + ny - 2)
 
     has = (gx > 0, gx < nx - 1, gy > 0, gy < ny - 1)
     to = (
@@ -211,6 +225,7 @@
     def take_k(i):
         stage_y(ST_K, i, K[i + 1])
     rows(take_k, ST_K)
+    send(ST_V)
 
     loads["map"].wait()
     loads["flags"].wait()
@@ -276,15 +291,14 @@
                 Pb[s + 1, i + 1] = new
                 stage_y(ST_P + s + 1, i, new)
         rows(low, ST_P + s + 1 if s + 1 < SUBSTEPS - 1 else None)
-        if s == 0:
-            send(ST_V)
+        if s == 1:
+            send(ST_U)
 
     def scatter(i):
         mean = FS[i][:, 0:1] * (1.0 / SUBSTEPS)
         AG[0, i] = jnp.sum(jnp.where(lane_gf == LK[i, :, 0:1], mean, 0.0), axis=0, keepdims=True)
     rows(scatter)
     fluxes = gather(AG, "gy", ny, gy, ag_s, ag_r)
-    send(ST_U)
 
     arrive(ST_K)
     loads["cap"].wait()

time: 55.1 us -> 53.5 us (0.971)
  Pallas kernels: 51.9 us -> 50.3 us
    pallas_call x1, Pallas kernels: 51.9 us -> 50.3 us  [local(): pl.pallas_call(functools.partial(kernel, nx, ny), out_shape=(jax.ShapeDty...]
where the time goes in v3:
time: 53.5 us; the launch traced here: 53.4 us
  Pallas kernels  50.3 us (94%)
  local copies, waits for them, and re-layouts  2.42 us (5%)
  between operations  0.65 us (1%)
    pallas_call x1, Pallas kernels, local(): pl.pallas_call(functools.partial(kernel, nx, ny), out_shape=(jax.ShapeDty...  50.3 us
    unnamed x4, local copies, waits for them, and re-layouts  2.42 us

profile of v3, /device:TPU:0, one launch (start us, length us, event | category | flops | bytes accessed | tf_op | source)
XLA Modules:
  0.0 53.4 jit_solution(7168751457122834429)
XLA Ops:
  0.6 50.3 %shard_map.104 = (f32[4,16,1024]{2,1,0:T(8,128)}, f32[4,16,1024]{2,1,0:T(8,128)}) custom-call(f32[4,16,1024]{2,1,0:T(8,128)} %u_hbm.1, f32[4,16,1024]{2,1,0:T(8,128)} %d_hbm.1, f32[3,4,16,1024]{3,2,1,0:T(8,128)} %c_hbm.1, s32[4,8,16]{2,1,0:T(8,128)} %bitcast.1, f32[4,16,1024]{2,1,0:T(8,128)} %v_hbm.1, f32[4,16,1024]{2,1,0:T(8,128)} %cap_hbm.1, ...), custom_call_target="tpu_custom_call" | custom-call | tf_op jit(solution)/shard_map/pallas_call | solution.py:501
  50.9 0.0 copy-start
  50.9 1.7 %copy.13 = f32[4,16,1024]{2,1,0:T(8,128)} copy(f32[4,16,1024]{2,1,0:T(8,128)} %get-tuple-element.4) | data formatting | bytes 524288
  52.6 0.0 copy-done
  52.7 0.7 %copy.14 = f32[4,16,1024]{2,1,0:T(8,128)} copy(f32[4,16,1024]{2,1,0:T(8,128)S(1)} %copy-done) | data formatting | bytes 524288
Async XLA Ops:
  50.9 1.7 %copy-start = (f32[4,16,1024]{2,1,0:T(8,128)S(1)}, f32[4,16,1024]{2,1,0:T(8,128)}, u32[]{:S(2)}) copy-start(f32[4,16,1024]{2,1,0:T(8,128)} %get-tuple-element.5) | copy-start | bytes 786436

commit v4 on v3

--- a/solution.py
+++ b/solution.py
@@ -26,15 +26,15 @@
 def kernel(
     nx, ny,
     u_hbm, d_hbm, c_hbm, flags_hbm, v_hbm, cap_hbm, k_hbm, heat_hbm, map_hbm,
-    u_out, v_out,
+    UO, VO,
     U, Pb, K, V, W,
     yU, yP, yK, yV, yW,
     sU, sP, sK, sV, sW,
     D, C, FLAGS, CAP, HEAT, MAP,
     CC, CXm, CXp, CYm, CYp, CZm, CZp, Q, GH, LK, FS,
     GX, GYm, GYp, GZm, GZp, DI, INV,
-    TG, AG, MU, MGY, MSX, MGX, UO, VO,
-    in_sem, out_sem, hs_sem, hr_sem, tg_s, tg_r, ag_s, ag_r, my_s, my_r, mx_s, mx_r,
+    TG, AG, MU, MGY, MSX, MGX,
+    in_sem, hs_sem, hr_sem, tg_s, tg_r, ag_s, ag_r, my_s, my_r, mx_s, mx_r,
 ):
     gx = lax.axis_index("gx")
     gy = lax.axis_index("gy")
@@ -418,8 +418,6 @@
     MGX[0] = jnp.broadcast_to(jnp.sum(total, axis=1, keepdims=True), total.shape)
     sums_x = gather(MGX, "gx", nx, gx, mx_s, mx_r)
     fluid_step(SUBSTEPS - 1)
-    out_u = pltpu.make_async_copy(UO, u_out, out_sem.at[0])
-    out_u.start()
     for cp in sums_x:
         cp.wait_recv()
     total = MGX[0]
@@ -456,15 +454,11 @@
             acc = acc + ys[j] * W[j, i + 1]
         VO[i] = acc
     rows(finish)
-    out_v = pltpu.make_async_copy(VO, v_out, out_sem.at[1])
-    out_v.start()
 
     for stage in range(STAGES):
         sent(stage)
     for cp in tops + fluxes + sums_y + sums_x:
         cp.wait_send()
-    out_u.wait()
-    out_v.wait()
 
 
 def solution(mesh):
@@ -491,21 +485,21 @@
         scratch += [vm(lx + 1, ly, zz)] + [vm(*field)] * 6
         scratch += [
             vm(ny, lx, 1, wg), vm(ny, lx, 1, wg), vm(2 * ITERS, LANES), vm(ny, 2 * ITERS, LANES),
-            vm(2 * ITERS, LANES), vm(nx, 2 * ITERS, LANES), vm(*field), vm(*field),
+            vm(2 * ITERS, LANES), vm(nx, 2 * ITERS, LANES),
         ]
         dma = lambda *shape: pltpu.SemaphoreType.DMA(shape)
         scratch += [
-            dma(9), dma(2), dma(STAGES, 4), dma(STAGES, 4),
+            dma(9), dma(STAGES, 4), dma(STAGES, 4),
             dma(ny), dma(ny), dma(ny), dma(ny), dma(ny), dma(ny), dma(nx), dma(nx),
         ]
         return pl.pallas_call(
             functools.partial(kernel, nx, ny),
-            out_shape=(jax.ShapeDtypeStruct(field, F32),) * 2,
+            out_shape=(pltpu.VMEM(field, F32),) * 2,
             in_specs=[pl.BlockSpec(memory_space=pltpu.HBM)] * 9,
-            out_specs=(pl.BlockSpec(memory_space=pl.ANY),) * 2,
+            out_specs=(pl.BlockSpec(memory_space=pltpu.VMEM),) * 2,
             scratch_shapes=scratch,
             compiler_params=pltpu.CompilerParams(
-                collective_id=0, has_side_effects=True, vmem_limit_bytes=67_000_000
+                collective_id=0, has_side_effects=True, vmem_limit_bytes=65000000
             ),
         )(u, d, c, jnp.swapaxes(flags, 1, 2), v, cap, k, heat, lookup)
 

time: 53.5 us -> 51.9 us (0.970)
  local copies, waits for them, and re-layouts: 2.42 us -> 1.41 us
  Pallas kernels: 50.3 us -> 49.7 us
    unnamed x4 -> x2, local copies, waits for them, and re-layouts: 2.42 us -> 1.41 us
    pallas_call x1, Pallas kernels: 50.3 us -> 49.7 us  [local(): pl.pallas_call(functools.partial(kernel, nx, ny), out_shape=(pltpu.VMEM(f...]
where the time goes in v4:
time: 51.9 us; the launch traced here: 51.7 us
  Pallas kernels  49.7 us (96%)
  local copies, waits for them, and re-layouts  1.41 us (3%)
  between operations  0.64 us (1%)
    pallas_call x1, Pallas kernels, local(): pl.pallas_call(functools.partial(kernel, nx, ny), out_shape=(pltpu.VMEM(f...  49.7 us
    unnamed x2, local copies, waits for them, and re-layouts  1.41 us

profile of v4, /device:TPU:0, one launch (start us, length us, event | category | flops | bytes accessed | tf_op | source)
XLA Modules:
  0.0 51.7 jit_solution(1077381388954664125)
XLA Ops:
  0.6 49.7 %shard_map.104 = (f32[4,16,1024]{2,1,0:T(8,128)S(1)}, f32[4,16,1024]{2,1,0:T(8,128)S(1)}) custom-call(f32[4,16,1024]{2,1,0:T(8,128)} %u_hbm.1, f32[4,16,1024]{2,1,0:T(8,128)} %d_hbm.1, f32[3,4,16,1024]{3,2,1,0:T(8,128)} %c_hbm.1, s32[4,8,16]{2,1,0:T(8,128)} %bitcast.1, f32[4,16,1024]{2,1,0:T(8,128)} %v_hbm.1, f32[4,16,1024]{2,1,0:T(8,128)} %cap_hbm.1, ...), custom_call_target="tpu_custom_call" | custom-call | tf_op jit(solution)/shard_map/pallas_call | solution.py:495
  50.3 0.7 %copy.13 = f32[4,16,1024]{2,1,0:T(8,128)} copy(f32[4,16,1024]{2,1,0:T(8,128)S(1)} %get-tuple-element.2) | data formatting | bytes 524288
  51.0 0.7 %copy.14 = f32[4,16,1024]{2,1,0:T(8,128)} copy(f32[4,16,1024]{2,1,0:T(8,128)S(1)} %get-tuple-element.3) | data formatting | bytes 524288
